TPU v7x, 32 devices: a whole 2x2x4 slice. The times are simulated.
32 devices in a mesh: slab: 8 (over z, y), batch: 4 (over x, core).
Axes of the slice: x: 2, y: 2, z: 4, core: 2. Of those that a mesh axis runs over, the one named last changes fastest.
Arguments:
- velocity_old: float32 [3, 16, 64, 128], P(None, 'slab', 'batch'), may hold values from -40 to 40
- courant: float32 [3, 16, 64, 128], P(None, 'slab', 'batch'), may hold values from -1.5 to 1.5
- cell_ids: int32 [32768], P(('slab', 'batch')), may hold values from 0 to 16383
- forces: float32 [3, 32768], P(None, ('slab', 'batch')), may hold values from -6 to 6
- weights: float32 [32768], P(('slab', 'batch')), may hold values from 0.25 to 4
Outputs:
- velocity_new: float32 [3, 16, 64, 128], P(None, 'slab', 'batch')
- residual: float32 [3, 16, 64, 128], P(None, 'slab', 'batch')
Inputs may be any that keep to these rules, and one draw needn't show every extreme that they name: `cell_ids`: each device's block of 1024 particles lists 1 * 128 particles for each destination slab in turn, slab 0 first.
All inputs are finite; a program needn't handle non-finite values.
Results may differ from a plain program's by a relative error of at most 0.0012.
Values may be sent and summed in bfloat16 or wider, within the bound.
No kernel may reach another device: no remote copies, remote signals or barrier semaphores. Data moves between devices by JAX's collectives and lax.ppermute only.
A program may use at most 64 MiB of HBM per device.

v0:
```python
import math
import jax
import jax.numpy as jnp
from jax import lax
from jax.sharding import PartitionSpec as P

ITERS = 2
diffusion_number = 1.0
diagonal_value = 7.0
deposit_block = 1024


def extended(block, sides, width):
    for axis, dim in sides:
        count = lax.axis_size(axis)
        forward = [(i, i + 1) for i in range(count - 1)]
        backward = [(target, source) for source, target in forward]
        low = lax.ppermute(
            lax.slice_in_dim(block, block.shape[dim] - width, None, axis=dim), axis, forward
        )
        high = lax.ppermute(lax.slice_in_dim(block, 0, width, axis=dim), axis, backward)
        block = jnp.concatenate([low, block, high], axis=dim)
    return block


def inner_product(left, right):
    return jnp.sum(left * right, axis=(1, 2, 3))


def expand(scalars):
    return scalars[:, None, None, None]


def factorize(upper_planes, lower_planes):
    inverses = []
    ratios = []
    for plane_index in range(len(upper_planes)):
        if plane_index == 0:
            pivot_value = diagonal_value + jnp.zeros_like(upper_planes[0])
        else:
            pivot_value = diagonal_value + lower_planes[plane_index] * ratios[-1]
        inverses.append(1.0 / pivot_value)
        ratios.append(-upper_planes[plane_index] * inverses[-1])
    return (inverses, ratios)


def solve_planes(value_planes, inverses, ratios, lower_planes):
    forward = []
    for plane_index in range(len(value_planes)):
        current = value_planes[plane_index]
        if plane_index > 0:
            current = current + lower_planes[plane_index] * forward[-1]
        forward.append(current * inverses[plane_index])
    result = [forward[-1]]
    plane_index = 0
    result.insert(0, forward[plane_index] - ratios[plane_index] * result[0])
    return result


def deposit_rows(cell_ids, momentum, row_total, planes, height, row_width):
    particle_count = cell_ids.shape[0]
    block_size = math.gcd(particle_count, deposit_block)
    row_range = lax.iota(jnp.int32, row_total)
    column_range = lax.iota(jnp.int32, row_width)

    def one_block(iteration, running):
        offset = iteration * block_size
        cell_part = lax.dynamic_slice_in_dim(cell_ids, offset, block_size, 0)
        momentum_part = lax.dynamic_slice_in_dim(momentum, offset, block_size, 1)
        plane_index = cell_part // (height * row_width)
        row_number = cell_part // row_width % height
        column = cell_part % row_width
        local_row = row_number * planes + plane_index
        row_hot = (local_row[:, None] == row_range[None, :]).astype(jnp.bfloat16)
        column_hot = column[:, None] == column_range[None, :]
        spread = jnp.where(
            column_hot[:, None, :], momentum_part.T[:, :, None], jnp.zeros((), jnp.bfloat16)
        )
        spread = spread.reshape(block_size, 3 * row_width)
        return running + jnp.einsum(
            "pr,pc->rc", row_hot, spread, preferred_element_type=jnp.float32
        )

    initial = jnp.zeros((row_total, 3 * row_width), jnp.float32)
    return lax.fori_loop(0, particle_count // block_size, one_block, initial)


def local(velocity_old, courant, cell_ids, forces, weights):
    planes = velocity_old.shape[1]
    rows_quarter = velocity_old.shape[2]
    row_width = velocity_old.shape[3]
    height = rows_quarter * lax.axis_size("batch")
    block_rows = planes * rows_quarter
    momentum = (weights[None, :] * forces).astype(jnp.bfloat16)
    ids_here = lax.all_to_all(cell_ids, "slab", split_axis=0, concat_axis=0, tiled=True)
    moved_momentum = lax.all_to_all(momentum, "slab", split_axis=1, concat_axis=1, tiled=True)
    summed = lax.psum_scatter(
        deposit_rows(
            ids_here, moved_momentum, block_rows * lax.axis_size("batch"), planes, height, row_width
        ),
        "batch",
        scatter_dimension=0,
        tiled=True,
    )
    source = summed.reshape(rows_quarter, planes, 3, row_width).transpose(2, 1, 0, 3)
    right_side = velocity_old + source
    upper = diffusion_number - 0.5 * courant
    lower = diffusion_number + 0.5 * courant
    upper_planes = [upper[0, plane_index] for plane_index in range(planes)]
    lower_planes = [lower[0, plane_index] for plane_index in range(planes)]
    inverses, ratios = factorize(upper_planes, lower_planes)

    def operate(values):
        padded = extended(values, (("slab", 1), ("batch", 2)), 1)
        edge_zeros = jnp.zeros_like(values[..., :1])
        plus_x = jnp.concatenate([values[..., 1:], edge_zeros], axis=3)
        minus_x = jnp.concatenate([edge_zeros, values[..., :-1]], axis=3)
        beside = upper[0] * padded[:, 2:, 1:-1] + lower[0] * padded[:, :-2, 1:-1]
        beside = beside + upper[1] * padded[:, 1:-1, 2:] + lower[1] * padded[:, 1:-1, :-2]
        beside = beside + upper[2] * plus_x + lower[2] * minus_x
        return diagonal_value * values - beside

    def precondition(values):
        value_planes = [values[:, plane_index] for plane_index in range(planes)]
        result = solve_planes(value_planes, inverses, ratios, lower_planes)
        return jnp.stack(result, axis=1)

    solution = jnp.zeros_like(right_side)
    residual = right_side
    direction = right_side
    rho_now = None
    for iteration in range(ITERS):
        precond_dir = precondition(direction)
        image_dir = operate(precond_dir)
        if iteration == 0:
            stacked_terms = jnp.stack(
                [inner_product(right_side, image_dir), inner_product(right_side, residual)], axis=0
            )
        else:
            stacked_terms = inner_product(right_side, image_dir)[None, :]
        gathered_sums = lax.psum(stacked_terms, ("slab", "batch"))
        along_sum = gathered_sums[0]
        if iteration == 0:
            rho_now = gathered_sums[1]
        step_alpha = rho_now / along_sum
        middle = residual - expand(step_alpha) * image_dir
        precond_mid = precondition(middle)
        turned = operate(precond_mid)
        term_list = [inner_product(turned, middle), inner_product(turned, turned)]
        if iteration + 1 < ITERS:
            term_list.append(inner_product(right_side, turned))
        closing_sums = lax.psum(jnp.stack(term_list, axis=0), ("slab", "batch"))
        cross_sum = closing_sums[0]
        square = closing_sums[1]
        shadow_turned = closing_sums[2] if iteration + 1 < ITERS else None
        step_omega = cross_sum / square
        solution = solution + expand(step_alpha) * precond_dir + expand(step_omega) * precond_mid
        residual = middle - expand(step_omega) * turned
        if iteration + 1 < ITERS:
            rho_next = rho_now - step_alpha * along_sum - step_omega * shadow_turned
            factor = rho_next / rho_now * (step_alpha / step_omega)
            direction = residual + expand(factor) * (direction - expand(step_omega) * image_dir)
            rho_now = rho_next
    return (solution, residual)


def solution(mesh):
    placed = (
        P(None, "slab", "batch", None),
        P(None, "slab", "batch", None),
        P(("slab", "batch")),
        P(None, ("slab", "batch")),
        P(("slab", "batch")),
    )
    return jax.shard_map(
        local,
        mesh=mesh,
        in_specs=placed,
        out_specs=(P(None, "slab", "batch", None), P(None, "slab", "batch", None)),
        check_vma=False,
    )
```

profile of v0, /device:TPU:0, one launch (start us, length us, event | category | flops | bytes accessed | tf_op | source)
XLA Modules:
  0.0 286.1 jit_solution(11093976552176510271)
XLA Ops:
  7.2 7.3 %all-to-all-start = ((s32[8,128,1]{1,2,0:T(1,128)}), s32[8,128,1]{1,2,0:T(1,128)S(1)}, u32[]{:S(2)}, u32[]{:S(2)}) async-start(s32[8,128,1]{1,2,0:T(1,128)} %bitcast.93), calls=%async_computation | async-start | bytes 8192 | tf_op jit(solution)/shard_map/all_to_all | solution.py:95
  14.5 0.0 copy-start.2
  14.5 0.8 multiply_add_fusion.2
  15.3 0.6 fusion.48
  16.0 5.0 %all-to-all-done = s32[8,128,1]{1,2,0:T(1,128)S(1)} async-done(((s32[8,128,1]{1,2,0:T(1,128)}), s32[8,128,1]{1,2,0:T(1,128)S(1)}, u32[]{:S(2)}, u32[]{:S(2)}) %all-to-all-start) | async-done | bytes 4128 | tf_op jit(solution)/shard_map/all_to_all | solution.py:95
  20.9 3.3 %all-to-all-start.1 = ((bf16[3,8,128]{2,0,1:T(4,128)(2,1)}), bf16[3,8,128]{2,0,1:T(4,128)(2,1)S(1)}, u32[]{:S(2)}, u32[]{:S(2)}) async-start(bf16[3,8,128]{2,0,1:T(4,128)(2,1)} %fusion.48), calls=%async_computation.1 | async-start | bytes 16384 | tf_op jit(solution)/shard_map/all_to_all | solution.py:96
  24.2 0.0 reduce-scatter.2.cloned.1.call-start
  24.3 0.1 iota_compare_fusion
  24.4 6.3 %all-to-all-done.1 = bf16[3,8,128]{2,0,1:T(4,128)(2,1)S(1)} async-done(((bf16[3,8,128]{2,0,1:T(4,128)(2,1)}), bf16[3,8,128]{2,0,1:T(4,128)(2,1)S(1)}, u32[]{:S(2)}, u32[]{:S(2)}) %all-to-all-start.1) | async-done | bytes 6176 | tf_op jit(solution)/shard_map/all_to_all | solution.py:96
  30.7 0.1 broadcast_select_fusion
  30.8 1.3 fusion.1
  32.1 0.0 reduce-scatter.2.cloned.1.call-update
  32.1 0.0 copy-start
  32.1 17.2 %reduce-scatter.2.cloned.1.call-done = f32[32,384]{1,0:T(8,128)} async-done(((f32[128,384]{1,0:T(8,128)}), f32[32,384]{1,0:T(8,128)}) %reduce-scatter.2.cloned.1.call-update) | async-done | bytes 49168 | tf_op jit(solution)/shard_map/reduce_scatter | solution.py:97
  49.3 0.8 reshape.219
  50.2 1.3 collective-permute-start
  51.5 4.5 %collective-permute-start.1 = (f32[3,1,16,128]{3,0,1,2:T(4,128)S(1)}, f32[3,1,16,128]{3,0,1,2:T(4,128)S(1)}, u32[]{:S(2)}, u32[]{:S(2)}) collective-permute-start(f32[3,1,16,128]{3,0,1,2:T(4,128)S(1)} %get-tuple-element.75), channel_id=1, source_target_pairs={{0,4},{4,8},{8,12},{12,16},{16,20},{20,24},{24,28},{1,5},{5,9},{9,... | collective-permute-start | bytes 73736 | tf_op jit(solution)/shard_map/ppermute | solution.py:18
  56.2 0.0 collective-permute-done
  56.2 1.4 collective-permute-done.1
  57.6 1.3 collective-permute-start.3
  58.9 1.3 collective-permute-start.2
  60.2 0.1 fusion.10
  60.3 0.0 collective-permute-done.3
  60.3 2.2 collective-permute-done.2
  62.5 0.2 multiply_reduce_fusion.7
  62.7 42.7 %psum.28 = f32[2,3]{1,0:T(2,128)S(1)} all-reduce(f32[2,3]{1,0:T(2,128)S(1)} %pad_maximum_fusion.53), channel_id=1, replica_groups=mesh['slab'=8,'batch'=4] {'slab','batch'}, use_global_device_ids=true, to_apply=%region_3.4 | all-reduce | flops 6 | bytes 48 | tf_op jit(solution)/shard_map/psum | solution.py:141
  105.4 0.1 multiply_subtract_fusion.3
  105.5 1.3 collective-permute-start.4
  106.8 4.8 %collective-permute-start.5 = (f32[3,1,16,128]{3,0,1,2:T(4,128)S(1)}, f32[3,1,16,128]{3,0,1,2:T(4,128)S(1)}, u32[]{:S(2)}, u32[]{:S(2)}) collective-permute-start(f32[3,1,16,128]{3,0,1,2:T(4,128)S(1)} %get-tuple-element.72), channel_id=1, source_target_pairs={{0,4},{4,8},{8,12},{12,16},{16,20},{20,24},{24,28},{1,5},{5,9},{9,... | collective-permute-start | bytes 73736 | tf_op jit(solution)/shard_map/ppermute | solution.py:18
  111.7 0.0 collective-permute-done.4
  111.7 1.6 collective-permute-done.5
  113.2 1.3 collective-permute-start.7
  114.5 1.3 collective-permute-start.6
  115.8 0.1 fusion.8
  115.9 3.9 %collective-permute-done.6 = f32[3,4,1,128]{3,0,1,2:T(4,128)S(1)} collective-permute-done((f32[3,4,1,128]{3,0,1,2:T(4,128)S(1)}, f32[3,4,1,128]{3,0,1,2:T(4,128)S(1)}, u32[]{:S(2)}, u32[]{:S(2)}) %collective-permute-start.6) | collective-permute-done | bytes 6176 | tf_op jit(solution)/shard_map/ppermute | solution.py:21
  119.9 0.3 multiply_reduce_fusion.5
  120.2 42.8 %psum.29 = f32[3,3]{1,0:T(4,128)S(1)} all-reduce(f32[3,3]{1,0:T(4,128)S(1)} %pad_maximum_fusion.52), channel_id=1, replica_groups=mesh['slab'=8,'batch'=4] {'slab','batch'}, use_global_device_ids=true, to_apply=%region_7.8 | all-reduce | flops 9 | bytes 72 | tf_op jit(solution)/shard_map/psum | solution.py:152
  163.0 0.1 multiply_add_fusion.1
  163.1 1.3 collective-permute-start.8
  164.4 4.8 %collective-permute-start.9 = (f32[3,1,16,128]{3,0,1,2:T(4,128)S(1)}, f32[3,1,16,128]{3,0,1,2:T(4,128)S(1)}, u32[]{:S(2)}, u32[]{:S(2)}) collective-permute-start(f32[3,1,16,128]{3,0,1,2:T(4,128)S(1)} %get-tuple-element.66), channel_id=1, source_target_pairs={{0,4},{4,8},{8,12},{12,16},{16,20},{20,24},{24,28},{1,5},{5,9},{9,... | collective-permute-start | bytes 73736 | tf_op jit(solution)/shard_map/ppermute | solution.py:18
  169.3 0.0 collective-permute-done.8
  169.3 1.6 collective-permute-done.9
  170.8 1.3 collective-permute-start.11
  172.1 1.3 collective-permute-start.10
  173.4 0.1 fusion.6
  173.5 0.0 collective-permute-done.11
  173.5 3.9 %collective-permute-done.10 = f32[3,4,1,128]{3,0,1,2:T(4,128)S(1)} collective-permute-done((f32[3,4,1,128]{3,0,1,2:T(4,128)S(1)}, f32[3,4,1,128]{3,0,1,2:T(4,128)S(1)}, u32[]{:S(2)}, u32[]{:S(2)}) %collective-permute-start.10) | collective-permute-done | bytes 6176 | tf_op jit(solution)/shard_map/ppermute | solution.py:21
  177.4 0.2 multiply_reduce_fusion.2
  177.7 42.8 %psum.30 = f32[3]{0:T(128)S(1)} all-reduce(f32[3]{0:T(128)S(1)} %get-tuple-element.63), channel_id=1, replica_groups=mesh['slab'=8,'batch'=4] {'slab','batch'}, use_global_device_ids=true, to_apply=%region_9.10 | all-reduce | flops 3 | bytes 24 | tf_op jit(solution)/shard_map/psum | solution.py:141
  220.4 0.1 multiply_subtract_fusion.1
  220.6 1.3 collective-permute-start.12
  221.9 4.8 %collective-permute-start.13 = (f32[3,1,16,128]{3,0,1,2:T(4,128)S(1)}, f32[3,1,16,128]{3,0,1,2:T(4,128)S(1)}, u32[]{:S(2)}, u32[]{:S(2)}) collective-permute-start(f32[3,1,16,128]{3,0,1,2:T(4,128)S(1)} %get-tuple-element.62), channel_id=1, source_target_pairs={{0,4},{4,8},{8,12},{12,16},{16,20},{20,24},{24,28},{1,5},{5,9},{9,... | collective-permute-start | bytes 73736 | tf_op jit(solution)/shard_map/ppermute | solution.py:18
  226.7 0.0 collective-permute-done.12
  226.7 1.6 collective-permute-done.13
  228.3 1.3 collective-permute-start.15
  229.6 1.3 collective-permute-start.14
  230.9 0.1 fusion.4
  231.0 0.0 collective-permute-done.15
  231.0 3.9 %collective-permute-done.14 = f32[3,4,1,128]{3,0,1,2:T(4,128)S(1)} collective-permute-done((f32[3,4,1,128]{3,0,1,2:T(4,128)S(1)}, f32[3,4,1,128]{3,0,1,2:T(4,128)S(1)}, u32[]{:S(2)}, u32[]{:S(2)}) %collective-permute-start.14) | collective-permute-done | bytes 6176 | tf_op jit(solution)/shard_map/ppermute | solution.py:21
  234.9 0.2 multiply_reduce_fusion.1
  235.1 42.7 %psum.31 = f32[2,3]{1,0:T(2,128)S(1)} all-reduce(f32[2,3]{1,0:T(2,128)S(1)} %pad_maximum_fusion.54), channel_id=1, replica_groups=mesh['slab'=8,'batch'=4] {'slab','batch'}, use_global_device_ids=true, to_apply=%region_12.13 | all-reduce | flops 6 | bytes 48 | tf_op jit(solution)/shard_map/psum | solution.py:152
  277.9 0.1 multiply_subtract_fusion
  278.0 0.6 copy.26
  278.7 0.6 copy.27
  (31 shorter events, 0.4 us)
Async XLA Ops:
  7.2 13.7 %all-to-all-start = ((s32[8,128,1]{1,2,0:T(1,128)}), s32[8,128,1]{1,2,0:T(1,128)S(1)}, u32[]{:S(2)}, u32[]{:S(2)}) async-start(s32[8,128,1]{1,2,0:T(1,128)} %bitcast.93), calls=%async_computation | async-start | bytes 8192 | tf_op jit(solution)/shard_map/all_to_all | solution.py:95
  14.5 0.8 copy-start.1
  14.5 0.8 copy-start.2
  20.9 9.8 %all-to-all-start.1 = ((bf16[3,8,128]{2,0,1:T(4,128)(2,1)}), bf16[3,8,128]{2,0,1:T(4,128)(2,1)S(1)}, u32[]{:S(2)}, u32[]{:S(2)}) async-start(bf16[3,8,128]{2,0,1:T(4,128)(2,1)} %fusion.48), calls=%async_computation.1 | async-start | bytes 16384 | tf_op jit(solution)/shard_map/all_to_all | solution.py:96
  24.2 25.0 %reduce-scatter.2.cloned.1.call-start = ((), (), s32[]{:S(2)}) async-start(), calls=%async_computation.3 | async-start | bytes 245760 | tf_op jit(solution)/shard_map/reduce_scatter | solution.py:97
  32.1 18.0 %copy-start = (f32[3,2,16,128]{3,2,1,0:T(8,128)S(1)}, f32[3,2,16,128]{3,2,1,0:T(8,128)}, u32[]{:S(2)}) copy-start(f32[3,2,16,128]{3,2,1,0:T(8,128)} %param.5) | copy-start | bytes 147460
  50.2 6.0 %collective-permute-start = (f32[3,1,16,128]{3,0,1,2:T(4,128)S(1)}, f32[3,1,16,128]{3,0,1,2:T(4,128)S(1)}, u32[]{:S(2)}, u32[]{:S(2)}) collective-permute-start(f32[3,1,16,128]{3,0,1,2:T(4,128)S(1)} %get-tuple-element.74), channel_id=1, source_target_pairs={{4,0},{8,4},{12,8},{16,12},{20,16},{24,20},{28,24},{5,1},{9,5},{13... | collective-permute-start | bytes 73736 | tf_op jit(solution)/shard_map/ppermute | solution.py:21
  51.5 6.1 %collective-permute-start.1 = (f32[3,1,16,128]{3,0,1,2:T(4,128)S(1)}, f32[3,1,16,128]{3,0,1,2:T(4,128)S(1)}, u32[]{:S(2)}, u32[]{:S(2)}) collective-permute-start(f32[3,1,16,128]{3,0,1,2:T(4,128)S(1)} %get-tuple-element.75), channel_id=1, source_target_pairs={{0,4},{4,8},{8,12},{12,16},{16,20},{20,24},{24,28},{1,5},{5,9},{9,... | collective-permute-start | bytes 73736 | tf_op jit(solution)/shard_map/ppermute | solution.py:18
  57.6 2.7 collective-permute-start.3
  58.9 3.6 %collective-permute-start.2 = (f32[3,4,1,128]{3,0,1,2:T(4,128)S(1)}, f32[3,4,1,128]{3,0,1,2:T(4,128)S(1)}, u32[]{:S(2)}, u32[]{:S(2)}) collective-permute-start(f32[3,4,1,128]{3,0,1,2:T(4,128)S(1)} %get-tuple-element.82), channel_id=1, source_target_pairs={{1,0},{2,1},{3,2},{5,4},{6,5},{7,6},{9,8},{10,9},{11,10},{13,12},{... | collective-permute-start | bytes 18440 | tf_op jit(solution)/shard_map/ppermute | solution.py:21
  105.5 6.1 %collective-permute-start.4 = (f32[3,1,16,128]{3,0,1,2:T(4,128)S(1)}, f32[3,1,16,128]{3,0,1,2:T(4,128)S(1)}, u32[]{:S(2)}, u32[]{:S(2)}) collective-permute-start(f32[3,1,16,128]{3,0,1,2:T(4,128)S(1)} %get-tuple-element.71), channel_id=1, source_target_pairs={{4,0},{8,4},{12,8},{16,12},{20,16},{24,20},{28,24},{5,1},{9,5},{13... | collective-permute-start | bytes 73736 | tf_op jit(solution)/shard_map/ppermute | solution.py:21
  106.8 6.4 %collective-permute-start.5 = (f32[3,1,16,128]{3,0,1,2:T(4,128)S(1)}, f32[3,1,16,128]{3,0,1,2:T(4,128)S(1)}, u32[]{:S(2)}, u32[]{:S(2)}) collective-permute-start(f32[3,1,16,128]{3,0,1,2:T(4,128)S(1)} %get-tuple-element.72), channel_id=1, source_target_pairs={{0,4},{4,8},{8,12},{12,16},{16,20},{20,24},{24,28},{1,5},{5,9},{9,... | collective-permute-start | bytes 73736 | tf_op jit(solution)/shard_map/ppermute | solution.py:18
  113.2 2.7 collective-permute-start.7
  114.5 5.3 %collective-permute-start.6 = (f32[3,4,1,128]{3,0,1,2:T(4,128)S(1)}, f32[3,4,1,128]{3,0,1,2:T(4,128)S(1)}, u32[]{:S(2)}, u32[]{:S(2)}) collective-permute-start(f32[3,4,1,128]{3,0,1,2:T(4,128)S(1)} %get-tuple-element.80), channel_id=1, source_target_pairs={{1,0},{2,1},{3,2},{5,4},{6,5},{7,6},{9,8},{10,9},{11,10},{13,12},{... | collective-permute-start | bytes 18440 | tf_op jit(solution)/shard_map/ppermute | solution.py:21
  163.1 6.1 %collective-permute-start.8 = (f32[3,1,16,128]{3,0,1,2:T(4,128)S(1)}, f32[3,1,16,128]{3,0,1,2:T(4,128)S(1)}, u32[]{:S(2)}, u32[]{:S(2)}) collective-permute-start(f32[3,1,16,128]{3,0,1,2:T(4,128)S(1)} %get-tuple-element.65), channel_id=1, source_target_pairs={{4,0},{8,4},{12,8},{16,12},{20,16},{24,20},{28,24},{5,1},{9,5},{13... | collective-permute-start | bytes 73736 | tf_op jit(solution)/shard_map/ppermute | solution.py:21
  164.4 6.4 %collective-permute-start.9 = (f32[3,1,16,128]{3,0,1,2:T(4,128)S(1)}, f32[3,1,16,128]{3,0,1,2:T(4,128)S(1)}, u32[]{:S(2)}, u32[]{:S(2)}) collective-permute-start(f32[3,1,16,128]{3,0,1,2:T(4,128)S(1)} %get-tuple-element.66), channel_id=1, source_target_pairs={{0,4},{4,8},{8,12},{12,16},{16,20},{20,24},{24,28},{1,5},{5,9},{9,... | collective-permute-start | bytes 73736 | tf_op jit(solution)/shard_map/ppermute | solution.py:18
  170.8 2.7 collective-permute-start.11
  172.1 5.3 %collective-permute-start.10 = (f32[3,4,1,128]{3,0,1,2:T(4,128)S(1)}, f32[3,4,1,128]{3,0,1,2:T(4,128)S(1)}, u32[]{:S(2)}, u32[]{:S(2)}) collective-permute-start(f32[3,4,1,128]{3,0,1,2:T(4,128)S(1)} %get-tuple-element.78), channel_id=1, source_target_pairs={{1,0},{2,1},{3,2},{5,4},{6,5},{7,6},{9,8},{10,9},{11,10},{13,12},{... | collective-permute-start | bytes 18440 | tf_op jit(solution)/shard_map/ppermute | solution.py:21
  220.6 6.1 %collective-permute-start.12 = (f32[3,1,16,128]{3,0,1,2:T(4,128)S(1)}, f32[3,1,16,128]{3,0,1,2:T(4,128)S(1)}, u32[]{:S(2)}, u32[]{:S(2)}) collective-permute-start(f32[3,1,16,128]{3,0,1,2:T(4,128)S(1)} %get-tuple-element.61), channel_id=1, source_target_pairs={{4,0},{8,4},{12,8},{16,12},{20,16},{24,20},{28,24},{5,1},{9,5},{13... | collective-permute-start | bytes 73736 | tf_op jit(solution)/shard_map/ppermute | solution.py:21
  221.9 6.4 %collective-permute-start.13 = (f32[3,1,16,128]{3,0,1,2:T(4,128)S(1)}, f32[3,1,16,128]{3,0,1,2:T(4,128)S(1)}, u32[]{:S(2)}, u32[]{:S(2)}) collective-permute-start(f32[3,1,16,128]{3,0,1,2:T(4,128)S(1)} %get-tuple-element.62), channel_id=1, source_target_pairs={{0,4},{4,8},{8,12},{12,16},{16,20},{20,24},{24,28},{1,5},{5,9},{9,... | collective-permute-start | bytes 73736 | tf_op jit(solution)/shard_map/ppermute | solution.py:18
  228.3 2.7 collective-permute-start.15
  229.6 5.3 %collective-permute-start.14 = (f32[3,4,1,128]{3,0,1,2:T(4,128)S(1)}, f32[3,4,1,128]{3,0,1,2:T(4,128)S(1)}, u32[]{:S(2)}, u32[]{:S(2)}) collective-permute-start(f32[3,4,1,128]{3,0,1,2:T(4,128)S(1)} %get-tuple-element.76), channel_id=1, source_target_pairs={{1,0},{2,1},{3,2},{5,4},{6,5},{7,6},{9,8},{10,9},{11,10},{13,12},{... | collective-permute-start | bytes 18440 | tf_op jit(solution)/shard_map/ppermute | solution.py:21
Sparse Core Ops, SparseCore 0:
  32.2 17.0 reduce-scatter.1
where the time goes:
time: 287 us; the launch traced here: 286 us
  blocking collectives  171 us (60%)
  waiting for transfers between devices  48.5 us (17%)
  starting transfers between devices  45.1 us (16%)
  between operations  14.5 us (5%)
  other arithmetic  3.66 us (1%)
    psum x2, blocking collectives, local(): closing_sums = lax.psum(jnp.stack(term_list, axis=0), ('slab', 'batch'))  85.6 us
    psum x2, blocking collectives, local(): gathered_sums = lax.psum(stacked_terms, ('slab', 'batch'))  85.4 us
    ppermute x8, starting transfers between devices, extended(): lax.ppermute(lax.slice_in_dim(block, block.shape[dim] - width, None, axis...  24.1 us
    reduce_scatter x1, waiting for transfers between devices, local(): lax.psum_scatter(deposit_rows(ids_here, moved_momentum, block_rows * lax....  17.2 us
    ppermute x8, waiting for transfers between devices, extended(): lax.ppermute(lax.slice_in_dim(block, 0, width, axis=dim), axis, backward)  13.9 us
    ppermute x8, starting transfers between devices, extended(): lax.ppermute(lax.slice_in_dim(block, 0, width, axis=dim), axis, backward)  10.3 us
    all_to_all x1, starting transfers between devices, local(): lax.all_to_all(cell_ids, 'slab', split_axis=0, concat_axis=0, tiled=True)  7.32 us
    all_to_all x1, waiting for transfers between devices, local(): lax.all_to_all(momentum, 'slab', split_axis=1, concat_axis=1, tiled=True)  6.3 us
  transfers between devices with their start and end apart: 19, of which 11 were waited for; matrix products, arithmetic and copies ran while one was open for 1% of the time, Pallas kernels for 0%

commit v1 on v0

--- a/solution.py
+++ b/solution.py
@@ -149,7 +149,7 @@
         term_list = [inner_product(turned, middle), inner_product(turned, turned)]
         if iteration + 1 < ITERS:
             term_list.append(inner_product(right_side, turned))
-        closing_sums = lax.psum(jnp.stack(term_list, axis=0), ("slab", "batch"))
+        closing_sums = lax.psum(lax.psum(jnp.stack(term_list, axis=0), "batch"), "slab")
         cross_sum = closing_sums[0]
         square = closing_sums[1]
         shadow_turned = closing_sums[2] if iteration + 1 < ITERS else None

time: 287 us -> 258 us (0.90)
  blocking collectives: 171 us -> 142 us
    psum x2 -> x4, blocking collectives: 85.6 us -> 58.7 us  [the longest x2 42.6 us: local(): lax.psum(lax.psum(jnp.stack(term_list, axis=0), 'batch'), 'slab')]
where the time goes in v1:
time: 258 us; the launch traced here: 257 us
  blocking collectives  142 us (55%)
  waiting for transfers between devices  48.1 us (19%)
  starting transfers between devices  44.8 us (17%)
  between operations  14.5 us (6%)
  other arithmetic  3.66 us (1%)
    psum x2, blocking collectives, local(): gathered_sums = lax.psum(stacked_terms, ('slab', 'batch'))  83.5 us
    psum x2, blocking collectives, local(): lax.psum(lax.psum(jnp.stack(term_list, axis=0), 'batch'), 'slab')  42.6 us
    ppermute x8, starting transfers between devices, extended(): lax.ppermute(lax.slice_in_dim(block, block.shape[dim] - width, None, axis...  23.8 us
    reduce_scatter x1, waiting for transfers between devices, local(): lax.psum_scatter(deposit_rows(ids_here, moved_momentum, block_rows * lax....  17.2 us
    psum x2, blocking collectives, local(): lax.psum(jnp.stack(term_list, axis=0), 'batch')  16.1 us
    ppermute x8, waiting for transfers between devices, extended(): lax.ppermute(lax.slice_in_dim(block, 0, width, axis=dim), axis, backward)  13.5 us
    ppermute x8, starting transfers between devices, extended(): lax.ppermute(lax.slice_in_dim(block, 0, width, axis=dim), axis, backward)  10.3 us
    all_to_all x1, starting transfers between devices, local(): lax.all_to_all(cell_ids, 'slab', split_axis=0, concat_axis=0, tiled=True)  7.32 us
  transfers between devices with their start and end apart: 19, of which 11 were waited for; matrix products, arithmetic and copies ran while one was open for 1% of the time, Pallas kernels for 0%

profile of v1, /device:TPU:0, one launch (start us, length us, event | category | flops | bytes accessed | tf_op | source)
XLA Modules:
  0.0 256.7 jit_solution(35111873674021365)
XLA Ops:
  7.2 7.3 %all-to-all-start = ((s32[8,128,1]{1,2,0:T(1,128)}), s32[8,128,1]{1,2,0:T(1,128)S(1)}, u32[]{:S(2)}, u32[]{:S(2)}) async-start(s32[8,128,1]{1,2,0:T(1,128)} %bitcast.93), calls=%async_computation | async-start | bytes 8192 | tf_op jit(solution)/shard_map/all_to_all | solution.py:95
  14.5 0.0 copy-start.2
  14.5 0.8 multiply_add_fusion.2
  15.3 0.6 fusion.48
  16.0 5.0 %all-to-all-done = s32[8,128,1]{1,2,0:T(1,128)S(1)} async-done(((s32[8,128,1]{1,2,0:T(1,128)}), s32[8,128,1]{1,2,0:T(1,128)S(1)}, u32[]{:S(2)}, u32[]{:S(2)}) %all-to-all-start) | async-done | bytes 4128 | tf_op jit(solution)/shard_map/all_to_all | solution.py:95
  20.9 3.3 %all-to-all-start.1 = ((bf16[3,8,128]{2,0,1:T(4,128)(2,1)}), bf16[3,8,128]{2,0,1:T(4,128)(2,1)S(1)}, u32[]{:S(2)}, u32[]{:S(2)}) async-start(bf16[3,8,128]{2,0,1:T(4,128)(2,1)} %fusion.48), calls=%async_computation.1 | async-start | bytes 16384 | tf_op jit(solution)/shard_map/all_to_all | solution.py:96
  24.2 0.0 reduce-scatter.2.cloned.1.call-start
  24.3 0.1 iota_compare_fusion
  24.4 6.3 %all-to-all-done.1 = bf16[3,8,128]{2,0,1:T(4,128)(2,1)S(1)} async-done(((bf16[3,8,128]{2,0,1:T(4,128)(2,1)}), bf16[3,8,128]{2,0,1:T(4,128)(2,1)S(1)}, u32[]{:S(2)}, u32[]{:S(2)}) %all-to-all-start.1) | async-done | bytes 6176 | tf_op jit(solution)/shard_map/all_to_all | solution.py:96
  30.7 0.1 broadcast_select_fusion
  30.8 1.3 fusion.1
  32.1 0.0 reduce-scatter.2.cloned.1.call-update
  32.1 0.0 copy-start
  32.1 17.2 %reduce-scatter.2.cloned.1.call-done = f32[32,384]{1,0:T(8,128)} async-done(((f32[128,384]{1,0:T(8,128)}), f32[32,384]{1,0:T(8,128)}) %reduce-scatter.2.cloned.1.call-update) | async-done | bytes 49168 | tf_op jit(solution)/shard_map/reduce_scatter | solution.py:97
  49.3 0.8 reshape.219
  50.2 1.3 collective-permute-start
  51.5 4.5 %collective-permute-start.1 = (f32[3,1,16,128]{3,0,1,2:T(4,128)S(1)}, f32[3,1,16,128]{3,0,1,2:T(4,128)S(1)}, u32[]{:S(2)}, u32[]{:S(2)}) collective-permute-start(f32[3,1,16,128]{3,0,1,2:T(4,128)S(1)} %get-tuple-element.75), channel_id=1, source_target_pairs={{0,4},{4,8},{8,12},{12,16},{16,20},{20,24},{24,28},{1,5},{5,9},{9,... | collective-permute-start | bytes 73736 | tf_op jit(solution)/shard_map/ppermute | solution.py:18
  56.2 0.0 collective-permute-done
  56.2 1.4 collective-permute-done.1
  57.6 1.3 collective-permute-start.3
  58.9 1.3 collective-permute-start.2
  60.2 0.1 fusion.10
  60.3 0.0 collective-permute-done.3
  60.3 2.2 collective-permute-done.2
  62.5 0.2 multiply_reduce_fusion.7
  62.7 42.6 %psum.42 = f32[2,3]{1,0:T(2,128)S(1)} all-reduce(f32[2,3]{1,0:T(2,128)S(1)} %pad_maximum_fusion.53), channel_id=1, replica_groups=mesh['slab'=8,'batch'=4] {'slab','batch'}, use_global_device_ids=true, to_apply=%region_3.4 | all-reduce | flops 6 | bytes 48 | tf_op jit(solution)/shard_map/psum | solution.py:141
  105.4 0.1 multiply_subtract_fusion.3
  105.5 1.3 collective-permute-start.4
  106.8 4.8 %collective-permute-start.5 = (f32[3,1,16,128]{3,0,1,2:T(4,128)S(1)}, f32[3,1,16,128]{3,0,1,2:T(4,128)S(1)}, u32[]{:S(2)}, u32[]{:S(2)}) collective-permute-start(f32[3,1,16,128]{3,0,1,2:T(4,128)S(1)} %get-tuple-element.72), channel_id=1, source_target_pairs={{0,4},{4,8},{8,12},{12,16},{16,20},{20,24},{24,28},{1,5},{5,9},{9,... | collective-permute-start | bytes 73736 | tf_op jit(solution)/shard_map/ppermute | solution.py:18
  111.6 0.0 collective-permute-done.4
  111.6 1.6 collective-permute-done.5
  113.2 1.3 collective-permute-start.7
  114.5 1.3 collective-permute-start.6
  115.8 0.1 fusion.8
  115.9 0.0 collective-permute-done.7
  115.9 3.9 %collective-permute-done.6 = f32[3,4,1,128]{3,0,1,2:T(4,128)S(1)} collective-permute-done((f32[3,4,1,128]{3,0,1,2:T(4,128)S(1)}, f32[3,4,1,128]{3,0,1,2:T(4,128)S(1)}, u32[]{:S(2)}, u32[]{:S(2)}) %collective-permute-start.6) | collective-permute-done | bytes 6176 | tf_op jit(solution)/shard_map/ppermute | solution.py:21
  119.8 0.3 multiply_reduce_fusion.5
  120.1 8.1 %psum.43 = f32[3,3]{1,0:T(4,128)S(1)} all-reduce(f32[3,3]{1,0:T(4,128)S(1)} %pad_maximum_fusion.52), channel_id=1, replica_groups=mesh['slab'=8,'batch'=4] {'batch'}, use_global_device_ids=true, to_apply=%region_7.8 | all-reduce | flops 9 | bytes 72 | tf_op jit(solution)/shard_map/psum | solution.py:152
  128.2 22.2 %psum.44 = f32[3,3]{1,0:T(4,128)S(1)} all-reduce(f32[3,3]{1,0:T(4,128)S(1)} %psum.43), channel_id=1, replica_groups=mesh['slab'=8,'batch'=4] {'slab'}, use_global_device_ids=true, to_apply=%region_8.9 | all-reduce | flops 9 | bytes 72 | tf_op jit(solution)/shard_map/psum | solution.py:152
  150.3 0.1 multiply_add_fusion.1
  150.5 1.3 collective-permute-start.8
  151.8 4.5 %collective-permute-start.9 = (f32[3,1,16,128]{3,0,1,2:T(4,128)S(1)}, f32[3,1,16,128]{3,0,1,2:T(4,128)S(1)}, u32[]{:S(2)}, u32[]{:S(2)}) collective-permute-start(f32[3,1,16,128]{3,0,1,2:T(4,128)S(1)} %get-tuple-element.66), channel_id=1, source_target_pairs={{0,4},{4,8},{8,12},{12,16},{16,20},{20,24},{24,28},{1,5},{5,9},{9,... | collective-permute-start | bytes 73736 | tf_op jit(solution)/shard_map/ppermute | solution.py:18
  156.3 0.0 collective-permute-done.8
  156.3 1.6 collective-permute-done.9
  157.9 1.3 collective-permute-start.11
  159.2 1.3 collective-permute-start.10
  160.5 0.1 fusion.6
  160.6 3.5 %collective-permute-done.10 = f32[3,4,1,128]{3,0,1,2:T(4,128)S(1)} collective-permute-done((f32[3,4,1,128]{3,0,1,2:T(4,128)S(1)}, f32[3,4,1,128]{3,0,1,2:T(4,128)S(1)}, u32[]{:S(2)}, u32[]{:S(2)}) %collective-permute-start.10) | collective-permute-done | bytes 6176 | tf_op jit(solution)/shard_map/ppermute | solution.py:21
  164.2 0.2 multiply_reduce_fusion.2
  164.4 40.9 %psum.45 = f32[3]{0:T(128)S(1)} all-reduce(f32[3]{0:T(128)S(1)} %get-tuple-element.63), channel_id=1, replica_groups=mesh['slab'=8,'batch'=4] {'slab','batch'}, use_global_device_ids=true, to_apply=%region_10.11 | all-reduce | flops 3 | bytes 24 | tf_op jit(solution)/shard_map/psum | solution.py:141
  205.3 0.1 multiply_subtract_fusion.1
  205.5 1.3 collective-permute-start.12
  206.8 4.8 %collective-permute-start.13 = (f32[3,1,16,128]{3,0,1,2:T(4,128)S(1)}, f32[3,1,16,128]{3,0,1,2:T(4,128)S(1)}, u32[]{:S(2)}, u32[]{:S(2)}) collective-permute-start(f32[3,1,16,128]{3,0,1,2:T(4,128)S(1)} %get-tuple-element.62), channel_id=1, source_target_pairs={{0,4},{4,8},{8,12},{12,16},{16,20},{20,24},{24,28},{1,5},{5,9},{9,... | collective-permute-start | bytes 73736 | tf_op jit(solution)/shard_map/ppermute | solution.py:18
  211.6 1.6 collective-permute-done.13
  213.2 1.3 collective-permute-start.15
  214.4 1.3 collective-permute-start.14
  215.7 0.1 fusion.4
  215.8 3.9 %collective-permute-done.14 = f32[3,4,1,128]{3,0,1,2:T(4,128)S(1)} collective-permute-done((f32[3,4,1,128]{3,0,1,2:T(4,128)S(1)}, f32[3,4,1,128]{3,0,1,2:T(4,128)S(1)}, u32[]{:S(2)}, u32[]{:S(2)}) %collective-permute-start.14) | collective-permute-done | bytes 6176 | tf_op jit(solution)/shard_map/ppermute | solution.py:21
  219.8 0.2 multiply_reduce_fusion.1
  220.0 8.1 %psum.46 = f32[2,3]{1,0:T(2,128)S(1)} all-reduce(f32[2,3]{1,0:T(2,128)S(1)} %pad_maximum_fusion.54), channel_id=1, replica_groups=mesh['slab'=8,'batch'=4] {'batch'}, use_global_device_ids=true, to_apply=%region_13.14 | all-reduce | flops 6 | bytes 48 | tf_op jit(solution)/shard_map/psum | solution.py:152
  228.1 20.4 %psum.47 = f32[2,3]{1,0:T(2,128)S(1)} all-reduce(f32[2,3]{1,0:T(2,128)S(1)} %psum.46), channel_id=1, replica_groups=mesh['slab'=8,'batch'=4] {'slab'}, use_global_device_ids=true, to_apply=%region_14.15 | all-reduce | flops 6 | bytes 48 | tf_op jit(solution)/shard_map/psum | solution.py:152
  248.5 0.1 multiply_subtract_fusion
  248.6 0.6 copy.26
  249.3 0.6 copy.27
  (33 shorter events, 0.4 us)
Async XLA Ops:
  7.2 13.7 %all-to-all-start = ((s32[8,128,1]{1,2,0:T(1,128)}), s32[8,128,1]{1,2,0:T(1,128)S(1)}, u32[]{:S(2)}, u32[]{:S(2)}) async-start(s32[8,128,1]{1,2,0:T(1,128)} %bitcast.93), calls=%async_computation | async-start | bytes 8192 | tf_op jit(solution)/shard_map/all_to_all | solution.py:95
  14.5 0.8 copy-start.1
  14.5 0.8 copy-start.2
  20.9 9.8 %all-to-all-start.1 = ((bf16[3,8,128]{2,0,1:T(4,128)(2,1)}), bf16[3,8,128]{2,0,1:T(4,128)(2,1)S(1)}, u32[]{:S(2)}, u32[]{:S(2)}) async-start(bf16[3,8,128]{2,0,1:T(4,128)(2,1)} %fusion.48), calls=%async_computation.1 | async-start | bytes 16384 | tf_op jit(solution)/shard_map/all_to_all | solution.py:96
  24.2 25.0 %reduce-scatter.2.cloned.1.call-start = ((), (), s32[]{:S(2)}) async-start(), calls=%async_computation.3 | async-start | bytes 245760 | tf_op jit(solution)/shard_map/reduce_scatter | solution.py:97
  32.1 18.0 %copy-start = (f32[3,2,16,128]{3,2,1,0:T(8,128)S(1)}, f32[3,2,16,128]{3,2,1,0:T(8,128)}, u32[]{:S(2)}) copy-start(f32[3,2,16,128]{3,2,1,0:T(8,128)} %param.5) | copy-start | bytes 147460
  50.2 6.0 %collective-permute-start = (f32[3,1,16,128]{3,0,1,2:T(4,128)S(1)}, f32[3,1,16,128]{3,0,1,2:T(4,128)S(1)}, u32[]{:S(2)}, u32[]{:S(2)}) collective-permute-start(f32[3,1,16,128]{3,0,1,2:T(4,128)S(1)} %get-tuple-element.74), channel_id=1, source_target_pairs={{4,0},{8,4},{12,8},{16,12},{20,16},{24,20},{28,24},{5,1},{9,5},{13... | collective-permute-start | bytes 73736 | tf_op jit(solution)/shard_map/ppermute | solution.py:21
  51.5 6.1 %collective-permute-start.1 = (f32[3,1,16,128]{3,0,1,2:T(4,128)S(1)}, f32[3,1,16,128]{3,0,1,2:T(4,128)S(1)}, u32[]{:S(2)}, u32[]{:S(2)}) collective-permute-start(f32[3,1,16,128]{3,0,1,2:T(4,128)S(1)} %get-tuple-element.75), channel_id=1, source_target_pairs={{0,4},{4,8},{8,12},{12,16},{16,20},{20,24},{24,28},{1,5},{5,9},{9,... | collective-permute-start | bytes 73736 | tf_op jit(solution)/shard_map/ppermute | solution.py:18
  57.6 2.7 %collective-permute-start.3 = (f32[3,4,1,128]{3,0,1,2:T(4,128)S(1)}, f32[3,4,1,128]{3,0,1,2:T(4,128)S(1)}, u32[]{:S(2)}, u32[]{:S(2)}) collective-permute-start(f32[3,4,1,128]{3,0,1,2:T(4,128)S(1)} %get-tuple-element.83), channel_id=1, source_target_pairs={{0,1},{1,2},{2,3},{4,5},{5,6},{6,7},{8,9},{9,10},{10,11},{12,13},{... | collective-permute-start | bytes 18440 | tf_op jit(solution)/shard_map/ppermute | solution.py:18
  58.9 3.6 %collective-permute-start.2 = (f32[3,4,1,128]{3,0,1,2:T(4,128)S(1)}, f32[3,4,1,128]{3,0,1,2:T(4,128)S(1)}, u32[]{:S(2)}, u32[]{:S(2)}) collective-permute-start(f32[3,4,1,128]{3,0,1,2:T(4,128)S(1)} %get-tuple-element.82), channel_id=1, source_target_pairs={{1,0},{2,1},{3,2},{5,4},{6,5},{7,6},{9,8},{10,9},{11,10},{13,12},{... | collective-permute-start | bytes 18440 | tf_op jit(solution)/shard_map/ppermute | solution.py:21
  105.5 6.1 %collective-permute-start.4 = (f32[3,1,16,128]{3,0,1,2:T(4,128)S(1)}, f32[3,1,16,128]{3,0,1,2:T(4,128)S(1)}, u32[]{:S(2)}, u32[]{:S(2)}) collective-permute-start(f32[3,1,16,128]{3,0,1,2:T(4,128)S(1)} %get-tuple-element.71), channel_id=1, source_target_pairs={{4,0},{8,4},{12,8},{16,12},{20,16},{24,20},{28,24},{5,1},{9,5},{13... | collective-permute-start | bytes 73736 | tf_op jit(solution)/shard_map/ppermute | solution.py:21
  106.8 6.4 %collective-permute-start.5 = (f32[3,1,16,128]{3,0,1,2:T(4,128)S(1)}, f32[3,1,16,128]{3,0,1,2:T(4,128)S(1)}, u32[]{:S(2)}, u32[]{:S(2)}) collective-permute-start(f32[3,1,16,128]{3,0,1,2:T(4,128)S(1)} %get-tuple-element.72), channel_id=1, source_target_pairs={{0,4},{4,8},{8,12},{12,16},{16,20},{20,24},{24,28},{1,5},{5,9},{9,... | collective-permute-start | bytes 73736 | tf_op jit(solution)/shard_map/ppermute | solution.py:18
  113.2 2.7 %collective-permute-start.7 = (f32[3,4,1,128]{3,0,1,2:T(4,128)S(1)}, f32[3,4,1,128]{3,0,1,2:T(4,128)S(1)}, u32[]{:S(2)}, u32[]{:S(2)}) collective-permute-start(f32[3,4,1,128]{3,0,1,2:T(4,128)S(1)} %get-tuple-element.81), channel_id=1, source_target_pairs={{0,1},{1,2},{2,3},{4,5},{5,6},{6,7},{8,9},{9,10},{10,11},{12,13},{... | collective-permute-start | bytes 18440 | tf_op jit(solution)/shard_map/ppermute | solution.py:18
  114.5 5.3 %collective-permute-start.6 = (f32[3,4,1,128]{3,0,1,2:T(4,128)S(1)}, f32[3,4,1,128]{3,0,1,2:T(4,128)S(1)}, u32[]{:S(2)}, u32[]{:S(2)}) collective-permute-start(f32[3,4,1,128]{3,0,1,2:T(4,128)S(1)} %get-tuple-element.80), channel_id=1, source_target_pairs={{1,0},{2,1},{3,2},{5,4},{6,5},{7,6},{9,8},{10,9},{11,10},{13,12},{... | collective-permute-start | bytes 18440 | tf_op jit(solution)/shard_map/ppermute | solution.py:21
  150.5 5.9 %collective-permute-start.8 = (f32[3,1,16,128]{3,0,1,2:T(4,128)S(1)}, f32[3,1,16,128]{3,0,1,2:T(4,128)S(1)}, u32[]{:S(2)}, u32[]{:S(2)}) collective-permute-start(f32[3,1,16,128]{3,0,1,2:T(4,128)S(1)} %get-tuple-element.65), channel_id=1, source_target_pairs={{4,0},{8,4},{12,8},{16,12},{20,16},{24,20},{28,24},{5,1},{9,5},{13... | collective-permute-start | bytes 73736 | tf_op jit(solution)/shard_map/ppermute | solution.py:21
  151.8 6.1 %collective-permute-start.9 = (f32[3,1,16,128]{3,0,1,2:T(4,128)S(1)}, f32[3,1,16,128]{3,0,1,2:T(4,128)S(1)}, u32[]{:S(2)}, u32[]{:S(2)}) collective-permute-start(f32[3,1,16,128]{3,0,1,2:T(4,128)S(1)} %get-tuple-element.66), channel_id=1, source_target_pairs={{0,4},{4,8},{8,12},{12,16},{16,20},{20,24},{24,28},{1,5},{5,9},{9,... | collective-permute-start | bytes 73736 | tf_op jit(solution)/shard_map/ppermute | solution.py:18
  157.9 2.7 %collective-permute-start.11 = (f32[3,4,1,128]{3,0,1,2:T(4,128)S(1)}, f32[3,4,1,128]{3,0,1,2:T(4,128)S(1)}, u32[]{:S(2)}, u32[]{:S(2)}) collective-permute-start(f32[3,4,1,128]{3,0,1,2:T(4,128)S(1)} %get-tuple-element.79), channel_id=1, source_target_pairs={{0,1},{1,2},{2,3},{4,5},{5,6},{6,7},{8,9},{9,10},{10,11},{12,13},{... | collective-permute-start | bytes 18440 | tf_op jit(solution)/shard_map/ppermute | solution.py:18
  159.2 5.0 %collective-permute-start.10 = (f32[3,4,1,128]{3,0,1,2:T(4,128)S(1)}, f32[3,4,1,128]{3,0,1,2:T(4,128)S(1)}, u32[]{:S(2)}, u32[]{:S(2)}) collective-permute-start(f32[3,4,1,128]{3,0,1,2:T(4,128)S(1)} %get-tuple-element.78), channel_id=1, source_target_pairs={{1,0},{2,1},{3,2},{5,4},{6,5},{7,6},{9,8},{10,9},{11,10},{13,12},{... | collective-permute-start | bytes 18440 | tf_op jit(solution)/shard_map/ppermute | solution.py:21
  205.5 6.1 %collective-permute-start.12 = (f32[3,1,16,128]{3,0,1,2:T(4,128)S(1)}, f32[3,1,16,128]{3,0,1,2:T(4,128)S(1)}, u32[]{:S(2)}, u32[]{:S(2)}) collective-permute-start(f32[3,1,16,128]{3,0,1,2:T(4,128)S(1)} %get-tuple-element.61), channel_id=1, source_target_pairs={{4,0},{8,4},{12,8},{16,12},{20,16},{24,20},{28,24},{5,1},{9,5},{13... | collective-permute-start | bytes 73736 | tf_op jit(solution)/shard_map/ppermute | solution.py:21
  206.8 6.4 %collective-permute-start.13 = (f32[3,1,16,128]{3,0,1,2:T(4,128)S(1)}, f32[3,1,16,128]{3,0,1,2:T(4,128)S(1)}, u32[]{:S(2)}, u32[]{:S(2)}) collective-permute-start(f32[3,1,16,128]{3,0,1,2:T(4,128)S(1)} %get-tuple-element.62), channel_id=1, source_target_pairs={{0,4},{4,8},{8,12},{12,16},{16,20},{20,24},{24,28},{1,5},{5,9},{9,... | collective-permute-start | bytes 73736 | tf_op jit(solution)/shard_map/ppermute | solution.py:18
  213.2 2.7 %collective-permute-start.15 = (f32[3,4,1,128]{3,0,1,2:T(4,128)S(1)}, f32[3,4,1,128]{3,0,1,2:T(4,128)S(1)}, u32[]{:S(2)}, u32[]{:S(2)}) collective-permute-start(f32[3,4,1,128]{3,0,1,2:T(4,128)S(1)} %get-tuple-element.77), channel_id=1, source_target_pairs={{0,1},{1,2},{2,3},{4,5},{5,6},{6,7},{8,9},{9,10},{10,11},{12,13},{... | collective-permute-start | bytes 18440 | tf_op jit(solution)/shard_map/ppermute | solution.py:18
  214.4 5.3 %collective-permute-start.14 = (f32[3,4,1,128]{3,0,1,2:T(4,128)S(1)}, f32[3,4,1,128]{3,0,1,2:T(4,128)S(1)}, u32[]{:S(2)}, u32[]{:S(2)}) collective-permute-start(f32[3,4,1,128]{3,0,1,2:T(4,128)S(1)} %get-tuple-element.76), channel_id=1, source_target_pairs={{1,0},{2,1},{3,2},{5,4},{6,5},{7,6},{9,8},{10,9},{11,10},{13,12},{... | collective-permute-start | bytes 18440 | tf_op jit(solution)/shard_map/ppermute | solution.py:21
Sparse Core Ops, SparseCore 0:
  32.2 17.0 reduce-scatter.1
